TPU v7x, 256 devices: a whole 4x4x8 slice. The times are simulated.
256 devices in a mesh: expert: 64 (over x, z, core), dp: 4 (over y).
Axes of the slice: x: 4, y: 4, z: 8, core: 2. Of those that a mesh axis runs over, the one named last changes fastest.
Arguments:
- sub_inputs: bfloat16 [32768, 4096], P(('expert', 'dp')), may hold values from -6 to 6
- out_grads: bfloat16 [32768, 4096], P(('expert', 'dp')), may hold values from -6 to 6
- expert_outputs: bfloat16 [32768, 4, 2, 1024], P(('expert', 'dp')), may hold values from -6 to 6
- combine_weights: float32 [32768, 4, 2], P(('expert', 'dp')), may hold values from 0.1 to 1
- expert_ids: int32 [32768, 4, 2], P(('expert', 'dp')), may hold values from 0 to 63, as said below
- slot_ids: int32 [32768, 4, 2], P(('expert', 'dp')), may hold values from -1 to 15, as said below
- expert_input_weight: bfloat16 [64, 1024, 1024], P('expert'), may hold values from -0.1875 to 0.1875
- expert_output_weight: bfloat16 [64, 1024, 1024], P('expert'), may hold values from -0.1875 to 0.1875
Outputs:
- d_inputs: bfloat16 [32768, 4096], P(('expert', 'dp'))
- d_gates: float32 [32768, 4, 2], P(('expert', 'dp'))
- dw_in: float32 [64, 1024, 1024], P('expert', 'dp')
- dw_out: float32 [64, 1024, 1024], P('expert', 'dp')
Inputs may be any that keep to these rules, and one draw needn't show every extreme that they name: `expert_ids`: the 2 experts of one sub-token differ. `slot_ids`: within the rows of one device, the kept entries that name one expert carry the slots 0, 1, 2, ... each once, so at most 16 of them; in every draw some expert has 16 kept entries from every device.
All inputs are finite; a program needn't handle non-finite values.
Results may differ from a plain program's by a relative error of at most 0.0085.
Values may be sent and summed in bfloat16 or wider, within the bound.
A program may use at most 128 MiB of HBM per device.

v0:
```python
import jax
import jax.numpy as jnp
from jax import lax
from jax.sharding import PartitionSpec as P


def in_one_piece(arrays, axis, split_dim, concat_dim, along):
    widths = [a.shape[along] for a in arrays]
    both = jnp.concatenate(arrays, axis=along)
    whole = lax.all_to_all(both, axis, split_axis=split_dim, concat_axis=concat_dim, tiled=True)
    return tuple(jnp.split(whole, [sum(widths[:k]) for k in range(1, len(widths))], axis=along))


def rounded(term):
    return lax.optimization_barrier(term.astype(jnp.bfloat16)).astype(jnp.float32)


def on_device(
    sub_inputs,
    out_grads,
    expert_outputs,
    combine_weights,
    expert_ids,
    slot_ids,
    expert_input_weight,
    expert_output_weight,
):
    token_count, head_count, top_count = expert_ids.shape
    local_count = expert_input_weight.shape[0]
    sub_width = expert_input_weight.shape[1]
    groups = lax.axis_size("expert")
    experts = groups * local_count
    capacity = top_count * head_count * token_count // experts
    name_count = token_count * head_count * top_count
    kept_mask = slot_ids.reshape(name_count) >= 0
    input_rows = sub_inputs.reshape(token_count * head_count, sub_width)
    grad_rows = out_grads.reshape(token_count * head_count, sub_width)
    output_rows = expert_outputs.reshape(token_count * head_count, top_count, sub_width)
    gate_dots = jnp.einsum("ns,nks->nk", grad_rows, output_rows, preferred_element_type=jnp.float32)
    d_gates = jnp.where(
        kept_mask.reshape(token_count, head_count, top_count),
        gate_dots.reshape(token_count, head_count, top_count),
        jnp.float32(0.0),
    )
    ids_flat = expert_ids.reshape(name_count)
    slots_flat = slot_ids.reshape(name_count)
    target = jnp.where(kept_mask, ids_flat * capacity + slots_flat, experts * capacity)
    owner_table = jnp.full((experts * capacity,), -1, jnp.int32)
    owner_table = owner_table.at[target].set(jnp.arange(name_count, dtype=jnp.int32), mode="drop")
    present = owner_table >= 0
    safe_index = jnp.maximum(owner_table, 0)
    source = safe_index // top_count
    send_inputs = jnp.where(present[:, None], input_rows[source], jnp.zeros((), jnp.bfloat16))
    scaled = combine_weights.reshape(name_count)[safe_index][:, None] * grad_rows[source].astype(
        jnp.float32
    )
    send_grads = jnp.where(present[:, None], scaled, jnp.float32(0.0)).astype(jnp.bfloat16)
    buffer_shape = (groups, local_count, capacity, sub_width)
    send_inputs = send_inputs.reshape(buffer_shape)
    send_grads = send_grads.reshape(buffer_shape)
    incoming_inputs, incoming_gradients = in_one_piece((send_inputs, send_grads), "expert", 0, 0, 1)
    preactivation_value = jnp.einsum(
        "qnrd,ndm->qnrm", incoming_inputs, expert_input_weight, preferred_element_type=jnp.float32
    )
    incoming_inputs, preactivation_value, hidden_activation = (
        incoming_inputs,
        preactivation_value,
        jax.nn.gelu(preactivation_value).astype(jnp.bfloat16),
    )
    hidden_grad = jnp.einsum(
        "uekx,ehx->uekh",
        incoming_gradients,
        expert_output_weight,
        preferred_element_type=jnp.float32,
    )
    _, gelu_back = jax.vjp(jax.nn.gelu, preactivation_value)
    preactivation_gradient = gelu_back(hidden_grad)[0].astype(jnp.bfloat16)
    input_grad = jnp.einsum(
        "arkz,roz->arko",
        preactivation_gradient,
        expert_input_weight,
        preferred_element_type=jnp.float32,
    ).astype(jnp.bfloat16)
    returned = lax.all_to_all(input_grad, "expert", split_axis=0, concat_axis=0, tiled=True)
    returned_rows = returned.reshape(experts * capacity, sub_width)
    gathered = returned_rows[jnp.where(kept_mask, target, 0)].astype(jnp.float32)
    merged = jnp.where(kept_mask[:, None], gathered, jnp.float32(0.0))
    merged = jnp.sum(merged.reshape(token_count * head_count, top_count, sub_width), axis=1)
    d_inputs = merged.astype(jnp.bfloat16).reshape(token_count, head_count * sub_width)
    grad_in_local = rounded(
        jnp.einsum(
            "pbqt,pbqn->btn",
            incoming_inputs,
            preactivation_gradient,
            preferred_element_type=jnp.float32,
        )
    )
    grad_out_local = rounded(
        jnp.einsum(
            "jmzw,jmzt->mwt",
            hidden_activation,
            incoming_gradients,
            preferred_element_type=jnp.float32,
        )
    )
    dw_in, dw_out = (
        lax.psum_scatter(
            grad_in_local.astype(jnp.bfloat16), "dp", scatter_dimension=1, tiled=True
        ).astype(jnp.float32),
        lax.psum_scatter(
            grad_out_local.astype(jnp.bfloat16), "dp", scatter_dimension=1, tiled=True
        ).astype(jnp.float32),
    )
    return (d_inputs, d_gates, dw_in, dw_out)


def solution(mesh):
    in_specs = (
        P(("expert", "dp"), None),
        P(("expert", "dp"), None),
        P(("expert", "dp"), None, None, None),
        P(("expert", "dp"), None, None),
        P(("expert", "dp"), None, None),
        P(("expert", "dp"), None, None),
        P("expert", None, None),
        P("expert", None, None),
    )
    out_specs = (
        P(("expert", "dp"), None),
        P(("expert", "dp"), None, None),
        P("expert", "dp", None),
        P("expert", "dp", None),
    )
    return jax.shard_map(
        on_device, mesh=mesh, in_specs=in_specs, out_specs=out_specs, check_vma=False
    )
```

profile of v0, /device:TPU:1, one launch (start us, length us, event | category | flops | bytes accessed | tf_op | source)
XLA Modules:
  0.0 269.8 jit_solution(5747871526038601578)
XLA Ops:
  7.2 1.8 reshape.203
  9.1 6.2 %reshape.265 = bf16[512,1024,1]{1,2,0:T(2,128)(2,1)} reshape(bf16[128,4096]{1,0:T(8,128)(2,1)} %param.9) | data formatting | bytes 2097152 | tf_op jit(solution)/shard_map/reshape | solution.py:37
  15.6 0.3 add.57
  15.9 6.5 %fusion.43 = f32[512,1,2]{2,1,0:T(1,128)S(1)} fusion(bf16[512,1024,1]{1,2,0:T(2,128)(2,1)} %reshape.265, bf16[512,2,1024]{2,1,0:T(2,128)(2,1)} %bitcast.126), kind=kOutput, calls=%fused_computation.65 | convolution fusion | flops 2097152 | bytes 3149824 | tf_op jit(solution)/shard_map/ns,nks->nk/dot_general | solution.py:39
  22.7 0.7 broadcast_select_fusion.1
  23.4 0.9 copy.39
  24.5 4.3 %scatter_custom_fusion = s32[1024]{0:T(1024)S(1)} fusion(s32[1024]{0:T(1024)S(1)} %bitcast.125, s32[1024]{0:T(1024)S(1)} %iota.3, s32[]{:T(128)} %constant.15.clone.1), kind=kCustom, calls=%fused_computation.59 | custom fusion | bytes 4100 | tf_op jit(solution)/shard_map/scatter | solution.py:49
  29.3 2.5 reshape.201
  31.8 4.5 %gather_fusion.1 = f32[1024]{0:T(1024)S(1)} fusion(f32[1024]{0:T(1024)S(1)} %reshape.202, s32[1024]{0:T(1024)S(1)} %get-tuple-element.16), kind=kCustom, calls=%fused_computation.1 | custom fusion | bytes 12288 | tf_op jit(solution)/shard_map/gather | solution.py:54
  36.4 5.4 %gather_fusion.2 = bf16[1024,1024]{1,0:T(8,128)(2,1)} fusion(bf16[512,1024]{1,0:T(8,128)(2,1)S(1)} %reshape.203, s32[1024]{0:T(1024)S(1)} %get-tuple-element.17), kind=kCustom, calls=%fused_computation.2 | custom fusion | bytes 4198400 | tf_op jit(solution)/shard_map/gather | solution.py:54
  41.8 7.4 %gather_fusion = bf16[1024,1024]{1,0:T(8,128)(2,1)} fusion(bf16[512,1024]{1,0:T(8,128)(2,1)} %reshape.201, s32[1024]{0:T(1024)S(1)} %get-tuple-element.17), kind=kCustom, calls=%fused_computation | custom fusion | bytes 4198400 | tf_op jit(solution)/shard_map/gather | solution.py:53
  49.2 2.0 broadcast_select_fusion
  51.4 0.6 fusion.8
  52.0 0.4 pad_maximum_fusion
  52.4 108.9 %all_to_all.10 = bf16[64,2,16,1024]{3,2,1,0:T(8,128)(2,1)S(1)} all-to-all(bf16[64,2,16,1024]{3,2,1,0:T(8,128)(2,1)S(1)} %pad_maximum_fusion), channel_id=1, replica_groups=mesh['expert'=64,'dp'=4] {'expert'}, dimensions={0} | all-to-all | bytes 8388608 | tf_op jit(solution)/shard_map/all_to_all | solution.py:10
  161.3 2.3 fusion.18
  163.7 0.8 copy-done.7
  164.4 4.7 %fusion.6 = bf16[64,1,16,1024]{3,2,0,1:T(8,128)(2,1)S(1)} fusion(f32[64,16,1024]{2,1,0:T(8,128)S(1)} %fusion.18, bf16[1,1024,1024]{2,1,0:T(8,128)(2,1)S(1)} %copy-done.7, bf16[64,2,16,1024]{3,2,1,0:T(8,128)(2,1)S(1)} %all_to_all.10), kind=kOutput, calls=%fused_computation.13 | convolution fusion | flops 2168455168 | bytes 10485760 | tf_op jit(solution)/shard_map/uekx,ehx->uekh/dot_general | solution.py:70
  169.2 1.3 copy-done.8
  170.5 3.8 %fusion.32 = bf16[1,1024,1024]{2,1,0:T(8,128)(2,1)} fusion(bf16[64,1,16,1024]{3,2,0,1:T(8,128)(2,1)S(1)} %fusion.6, bf16[64,2,16,1024]{3,2,1,0:T(8,128)(2,1)S(1)} %all_to_all.10), kind=kOutput, calls=%fused_computation.44 | convolution fusion | flops 2148532224 | bytes 6291456 | tf_op jit(solution)/shard_map/pbqt,pbqn->btn/dot_general | solution.py:91
  174.3 5.3 %convert_bitcast_fusion = bf16[64,1,16,1024]{3,2,1,0:T(8,128)(2,1)} fusion(bf16[1,1024,1024]{2,1,0:T(8,128)(2,1)S(1)} %copy-done, bf16[64,1,16,1024]{3,2,0,1:T(8,128)(2,1)} %copy-done.8), kind=kOutput, calls=%fused_computation.38 | convolution fusion | flops 2148532224 | bytes 6291456 | tf_op jit(solution)/shard_map/arkz,roz->arko/dot_general | solution.py:78
  179.6 6.0 %all-to-all-start.1 = ((bf16[64,1,16,1024]{3,2,1,0:T(8,128)(2,1)}), bf16[64,1,16,1024]{3,2,1,0:T(8,128)(2,1)}, u32[]{:S(2)}, u32[]{:S(2)}) async-start(bf16[64,1,16,1024]{3,2,1,0:T(8,128)(2,1)} %convert_bitcast_fusion), calls=%async_computation.1 | async-start | bytes 4194304 | tf_op jit(solution)/shard_map/all_to_all | solution.py:84
  185.6 0.3 reduce-scatter.5.cloned.1.call-start
  185.9 7.0 %fusion.29 = bf16[1,1024,1024]{2,1,0:T(8,128)(2,1)} fusion(bf16[64,2,16,1024]{3,2,1,0:T(8,128)(2,1)} %copy-done.2, f32[64,16,1024]{2,1,0:T(8,128)} %copy-done.9), kind=kOutput, calls=%fused_computation.43 | convolution fusion | flops 2157969408 | bytes 8388608 | tf_op jit(solution)/shard_map/jmzw,jmzt->mwt/dot_general | solution.py:99
  192.9 0.7 copy.36
  193.6 43.1 %all-to-all-done.1 = bf16[64,1,16,1024]{3,2,1,0:T(8,128)(2,1)} async-done(((bf16[64,1,16,1024]{3,2,1,0:T(8,128)(2,1)}), bf16[64,1,16,1024]{3,2,1,0:T(8,128)(2,1)}, u32[]{:S(2)}, u32[]{:S(2)}) %all-to-all-start.1) | async-done | bytes 2097184 | tf_op jit(solution)/shard_map/all_to_all | solution.py:84
  236.8 7.9 %gather_fusion.3 = bf16[1024,1024]{1,0:T(8,128)(2,1)} fusion(bf16[1024,1024]{1,0:T(8,128)(2,1)} %bitcast.27, s32[1024]{0:T(1024)S(1)} %broadcast_clamp_fusion), kind=kCustom, calls=%fused_computation.3 | custom fusion | bytes 4198400 | tf_op jit(solution)/shard_map/gather | solution.py:86
  244.7 5.5 %reshape.214 = f32[512,2,1024]{2,1,0:T(2,128)} reshape(bf16[1024,1024]{1,0:T(8,128)(2,1)} %gather_fusion.3) | data formatting | bytes 6291456 | tf_op jit(solution)/shard_map/convert_element_type | solution.py:86
  250.1 7.1 %select_reduce_fusion = bf16[512,1024]{1,0:T(8,128)(2,1)S(1)} fusion(f32[512,2,1024]{2,1,0:T(2,128)} %reshape.214, pred[512,2]{1,0:T(8,128)(4,1)S(1)} %bitcast.122), kind=kLoop, calls=%fused_computation.27 | loop fusion | flops 1572864 | bytes 5243904 | tf_op jit(solution)/shard_map/reduce_sum | solution.py:88
  257.2 1.5 convert_element_type.88
  258.7 2.1 convert_element_type.91
  260.8 2.1 convert_element_type.95
  (38 shorter events, 1.8 us)
Async XLA Ops:
  7.2 154.1 %copy-start = (bf16[1,1024,1024]{2,1,0:T(8,128)(2,1)S(1)}, bf16[1,1024,1024]{2,1,0:T(8,128)(2,1)}, u32[]{:S(2)}) copy-start(bf16[1,1024,1024]{2,1,0:T(8,128)(2,1)} %param.14) | copy-start | bytes 6291460
  7.2 8.1 %copy-start.4 = (s32[128,4,2]{0,2,1:T(2,128)S(1)}, s32[128,4,2]{0,2,1:T(2,128)}, u32[]{:S(2)}) copy-start(s32[128,4,2]{0,2,1:T(2,128)} %param.13) | copy-start | bytes 12292
  7.2 8.2 %copy-start.6 = (s32[128,4,2]{0,2,1:T(2,128)S(1)}, s32[128,4,2]{0,2,1:T(2,128)}, u32[]{:S(2)}) copy-start(s32[128,4,2]{0,2,1:T(2,128)} %param.12) | copy-start | bytes 12292
  7.2 251.5 %reduce-scatter.3.cloned.1.call-start = ((), (), s32[]{:S(2)}) async-start(), calls=%async_computation.4 | async-start | bytes 2621440 | tf_op jit(solution)/shard_map/reduce_scatter | solution.py:107
  15.9 12.9 %copy-start.5 = (f32[128,4,2]{0,2,1:T(2,128)S(1)}, f32[128,4,2]{0,2,1:T(2,128)}, u32[]{:S(2)}) copy-start(f32[128,4,2]{0,2,1:T(2,128)} %param.11) | copy-start | bytes 12292
  49.2 2.2 copy-start.1
  161.3 7.9 %copy-start.2 = (bf16[64,2,16,1024]{3,2,1,0:T(8,128)(2,1)}, bf16[64,2,16,1024]{3,2,1,0:T(8,128)(2,1)S(1)}, u32[]{:S(2)}) copy-start(bf16[64,2,16,1024]{3,2,1,0:T(8,128)(2,1)S(1)} %all_to_all.10) | copy-start | bytes 12582916
  161.3 3.1 %copy-start.7 = (bf16[1,1024,1024]{2,1,0:T(8,128)(2,1)S(1)}, bf16[1,1024,1024]{2,1,0:T(8,128)(2,1)}, u32[]{:S(2)}) copy-start(bf16[1,1024,1024]{2,1,0:T(8,128)(2,1)} %param.15) | copy-start | bytes 6291460
  164.4 4.8 %copy-start.9 = (f32[64,16,1024]{2,1,0:T(8,128)}, f32[64,16,1024]{2,1,0:T(8,128)S(1)}, u32[]{:S(2)}) copy-start(f32[64,16,1024]{2,1,0:T(8,128)S(1)} %fusion.18) | copy-start | bytes 12582916
  169.2 1.3 copy-start.8
  179.6 57.1 %all-to-all-start.1 = ((bf16[64,1,16,1024]{3,2,1,0:T(8,128)(2,1)}), bf16[64,1,16,1024]{3,2,1,0:T(8,128)(2,1)}, u32[]{:S(2)}, u32[]{:S(2)}) async-start(bf16[64,1,16,1024]{3,2,1,0:T(8,128)(2,1)} %convert_bitcast_fusion), calls=%async_computation.1 | async-start | bytes 4194304 | tf_op jit(solution)/shard_map/all_to_all | solution.py:84
  185.6 7.3 %copy-start.3 = (f32[128,4,2]{1,0,2:T(8,128)S(1)}, f32[128,4,2]{1,0,2:T(8,128)}, u32[]{:S(2)}) copy-start(f32[128,4,2]{1,0,2:T(8,128)} %get-tuple-element.12) | copy-start | bytes 12292
  185.6 75.2 %reduce-scatter.5.cloned.1.call-start = ((), (), s32[]{:S(2)}) async-start(), calls=%async_computation.5 | async-start | bytes 2621440 | tf_op jit(solution)/shard_map/reduce_scatter | solution.py:110
Sparse Core Ops, SparseCore 0:
  174.5 28.8 reduce-scatter.2
  205.9 31.9 reduce-scatter.4
where the time goes:
time: 271 us; the launch traced here: 270 us
  blocking collectives  109 us (40%)
  local copies, waits for them, and re-layouts  52.4 us (19%)
  waiting for transfers between devices  43.2 us (16%)
  matrix products  29.6 us (11%)
  other arithmetic  15 us (6%)
  between operations  14.3 us (5%)
  starting transfers between devices  6.32 us (2%)
    all_to_all x1, blocking collectives, in_one_piece(): lax.all_to_all(both, axis, split_axis=split_dim, concat_axis=concat_dim,...  109 us
    all_to_all x1, waiting for transfers between devices, on_device(): lax.all_to_all(input_grad, 'expert', split_axis=0, concat_axis=0, tiled=T...  43.1 us
    reshape x2, local copies, waits for them, and re-layouts, on_device(): grad_rows = out_grads.reshape(token_count * head_count, sub_width)  8.01 us
    gather x1, local copies, waits for them, and re-layouts, on_device(): returned_rows[jnp.where(kept_mask, target, 0)].astype(jnp.float32)  7.9 us
    gather x1, local copies, waits for them, and re-layouts, on_device(): input_rows[source]  7.36 us
    reduce_sum x1, other arithmetic, on_device(): jnp.sum(merged.reshape(token_count * head_count, top_count, sub_width), a...  7.13 us
    dot_general x1, matrix products, on_device(): jnp.einsum('jmzw,jmzt->mwt', hidden_activation, incoming_gradients, prefe...  6.99 us
    dot_general x1, matrix products, on_device(): jnp.einsum('ns,nks->nk', grad_rows, output_rows, preferred_element_type=j...  6.51 us
  transfers between devices with their start and end apart: 3, of which 1 were waited for; matrix products, arithmetic and copies ran while one was open for 14% of the time, Pallas kernels for 0%

commit v1 on v0

v1 whole, which is shorter than its diff:
```python
import functools
import math

import jax
import jax.numpy as jnp
from jax import lax
from jax.experimental import pallas as pl
from jax.experimental.pallas import tpu as pltpu
from jax.sharding import PartitionSpec as P

MESH = pl.DeviceIdType.MESH
NX, NZ, NC = 4, 8, 2
NY = 4
CAP = 16
PEERS = NX * NC
ROWS = PEERS * CAP
GELU_C = math.sqrt(2.0 / math.pi)
NT = (((1,), (1,)), ((), ()))
TN = (((0,), (0,)), ((), ()))
F32, BF16 = jnp.float32, jnp.bfloat16


def kernel(
    x_hbm, g_hbm, eo_hbm, w_ref, ids_ref, slots_ref, w1_hbm, w2_hbm,
    din_ref, dgate_ref, dwin_ref, dwout_ref,
    xs, gs, eo, w1, w2, tgt, onehot, send, recv, hid, grad, rsend, rrecv, acc,
    part, opp, fwd, direct,
    load_sem, send_sem, recv_sem, rsend_sem, rrecv_sem, y_send, y_opp, y_dir,
):
    sub = w1.shape[0]
    tok = xs.shape[0] // 4
    e, y = lax.axis_index("expert"), lax.axis_index("dp")
    x, z, c = e // (NZ * NC), lax.rem(e // NC, NZ), lax.rem(e, NC)
    up, down = lax.rem(y + 1, NY), lax.rem(y + NY - 1, NY)

    loads = []
    for src, dst, k in ((x_hbm, xs, 0), (g_hbm, gs, 1)):
        for h in range(4):
            loads.append(
                pltpu.make_async_copy(
                    src.at[:, h * sub:(h + 1) * sub], dst.at[pl.ds(h * tok, tok)], load_sem.at[k, h]
                )
            )
    late = [
        pltpu.make_async_copy(w1_hbm, w1, load_sem.at[2, 0]),
        pltpu.make_async_copy(w2_hbm, w2, load_sem.at[2, 1]),
        pltpu.make_async_copy(eo_hbm, eo, load_sem.at[2, 2]),
    ]
    for copy in loads + late:
        copy.start()

    barrier = pltpu.get_barrier_semaphore()

    def greet(k, _):
        pl.semaphore_signal(barrier, inc=1, device_id=(lax.rem(e + k, NX * NZ * NC), y), device_id_type=MESH)
        return 0

    lax.fori_loop(1, NX * NZ * NC, greet, 0)
    for other in (up, down):
        pl.semaphore_signal(barrier, inc=1, device_id=(e, other), device_id_type=MESH)

    tgt[...] = jnp.where(slots_ref[...] >= 0, ids_ref[...] * CAP + slots_ref[...], -1)

    def offset_z(j):
        half = (j + 1) // 2
        return lax.rem(NZ // 2 + half * (1 - 2 * lax.rem(j, 2)), NZ)

    def build(j):
        dz = offset_z(j)
        row = lax.broadcasted_iota(jnp.int32, (ROWS, tok), 0)
        px = (x + (row >> 5)) & (NX - 1)
        pz = lax.rem(z + dz, NZ)
        pc = (c + ((row >> 4) & 1)) & 1
        slot = (((px * NZ) + pz) * NC + pc) * CAP + (row & (CAP - 1))
        scale = jnp.zeros((ROWS, tok), F32)
        for h in range(4):
            first = tgt[h, 0:1, :] == slot
            second = tgt[h, 1:2, :] == slot
            onehot[j, :, h * tok:(h + 1) * tok] = jnp.where(first | second, 1.0, 0.0).astype(BF16)
            scale = scale + jnp.where(first, w_ref[h, 0:1, :], 0.0) + jnp.where(second, w_ref[h, 1:2, :], 0.0)
        scale = jnp.sum(scale, axis=1, keepdims=True)
        pick = onehot[j]
        rows_x = jnp.dot(pick, xs[...], preferred_element_type=F32).astype(BF16)
        rows_g = (jnp.dot(pick, gs[...], preferred_element_type=F32) * scale).astype(BF16)
        send[j, :, 0] = rows_x.reshape(PEERS, CAP, sub)
        send[j, :, 1] = rows_g.reshape(PEERS, CAP, sub)

    def peer(j, i, sign):
        dz, dx, dc = offset_z(j), i // NC, i % NC
        px = lax.rem(x + NX + sign * dx, NX)
        pz = lax.rem(z + NZ + sign * dz, NZ)
        return ((px * NZ) + pz) * NC + lax.rem(c + dc, NC)

    def out_copy(j, i):
        return pltpu.make_async_remote_copy(
            src_ref=send.at[j, i], dst_ref=recv.at[j, i], send_sem=send_sem.at[j], recv_sem=recv_sem.at[j],
            device_id=(peer(j, i, 1), y), device_id_type=MESH,
        )

    def back_copy(j, i):
        return pltpu.make_async_remote_copy(
            src_ref=rsend.at[j, i], dst_ref=rrecv.at[j, i], send_sem=rsend_sem.at[j], recv_sem=rrecv_sem.at[j],
            device_id=(peer(j, i, -1), y), device_id_type=MESH,
        )

    last = NZ - 1

    def ship(j, copy):
        @pl.when(j < last)
        def _():
            copy(j, 0).start()

        for i in range(1, PEERS):
            copy(j, i).start()

    def settle(j, buf, sem):
        @pl.when(j < last)
        def _():
            pltpu.make_async_copy(buf.at[j], buf.at[j], sem.at[j]).wait()

        @pl.when(j == last)
        def _():
            own = buf.at[j, pl.ds(1, PEERS - 1)]
            pltpu.make_async_copy(own, own, sem.at[j]).wait()

    for copy in loads:
        copy.wait()
    build(0)
    pl.semaphore_wait(barrier, NX * NZ * NC - 1 + 2)

    def dispatch(j, _):
        build(j)
        ship(j - 1, out_copy)
        return 0

    lax.fori_loop(1, NZ, dispatch, 0)
    recv[last, 0] = send[last, 0]
    ship(last, out_copy)

    late[2].wait()
    for h in range(4):
        mine = eo[:, h].reshape(2 * tok, sub)
        dots = lax.dot_general(mine, gs[h * tok:(h + 1) * tok, :], NT, preferred_element_type=F32)
        row = lax.broadcasted_iota(jnp.int32, (2 * tok, tok), 0)
        col = lax.broadcasted_iota(jnp.int32, (2 * tok, tok), 1)
        for k in range(2):
            kept = jnp.sum(jnp.where(row == 2 * col + k, dots, 0.0), axis=0, keepdims=True)
            dgate_ref[h, k:k + 1, :] = jnp.where(slots_ref[h, k:k + 1, :] >= 0, kept, 0.0)
    late[0].wait()
    late[1].wait()

    def experts(j, _):
        settle(j, recv, recv_sem)
        rows_x = recv[j, :, 0].reshape(ROWS, sub)
        rows_g = recv[j, :, 1].reshape(ROWS, sub)
        v = jnp.dot(rows_x, w1[...], preferred_element_type=F32)
        d = lax.dot_general(rows_g, w2[...], NT, preferred_element_type=F32)
        square = v * v
        t = jnp.tanh(GELU_C * (v + 0.044715 * (square * v)))
        cdf = 0.5 * (1.0 + t)
        slope = cdf + (0.5 * v) * (1.0 - t * t) * (GELU_C * (1.0 + (3 * 0.044715) * square))
        f = (d * slope).astype(BF16)
        r = lax.dot_general(f, w1[...], NT, preferred_element_type=F32).astype(BF16)
        rsend[j] = r.reshape(PEERS, CAP, sub)
        at = pl.ds(pl.multiple_of(j * ROWS, ROWS), ROWS)
        grad[at, :] = f
        hid[at, :] = (v * cdf).astype(BF16)
        ship(j, back_copy)
        return 0

    lax.fori_loop(0, NZ, experts, 0)
    rrecv[last, 0] = rsend[last, 0]

    quarter = sub // NY
    half = quarter // 2

    def quarter_of(a, k):
        cols = pl.ds(pl.multiple_of(lax.rem(y + k, NY) * quarter, quarter), quarter)
        if a == 0:
            left, right = hid[:, cols], recv[:, :, 1].reshape(NZ * ROWS, sub)
        else:
            left, right = recv[:, :, 0, :, cols].reshape(NZ * ROWS, quarter), grad[...]
        part[a, k] = lax.dot_general(left, right, TN, preferred_element_type=F32).astype(BF16)

    def along(src, dst, s_sem, r_sem, to):
        return pltpu.make_async_remote_copy(
            src_ref=src, dst_ref=dst, send_sem=s_sem, recv_sem=r_sem, device_id=(e, to), device_id_type=MESH
        )

    ups, downs = pl.ds(0, half), pl.ds(half, half)
    first_up = [along(part.at[a, 2, ups], opp.at[a, 0], y_send.at[0, a], y_opp.at[a, 0], up) for a in range(2)]
    first_down = [along(part.at[a, 2, downs], opp.at[a, 1], y_send.at[1, a], y_opp.at[a, 1], down) for a in range(2)]
    plain_up = [along(part.at[a, 1, downs], direct.at[a, 0, downs], y_send.at[2, a], y_dir.at[a, 0], up) for a in range(2)]
    plain_down = [along(part.at[a, 3, ups], direct.at[a, 1, ups], y_send.at[3, a], y_dir.at[a, 1], down) for a in range(2)]
    second_up = [along(fwd.at[a, 0], direct.at[a, 0, ups], y_send.at[4, a], y_dir.at[a, 2], up) for a in range(2)]
    second_down = [along(fwd.at[a, 1], direct.at[a, 1, downs], y_send.at[5, a], y_dir.at[a, 3], down) for a in range(2)]

    quarter_of(0, 2)
    quarter_of(1, 2)
    for a in range(2):
        first_up[a].start()
        first_down[a].start()
    for k in (1, 3):
        for a in range(2):
            quarter_of(a, k)
    for a in range(2):
        plain_up[a].start()
        plain_down[a].start()
    for a in range(2):
        quarter_of(a, 0)
    for a in range(2):
        first_up[a].wait_recv()
        fwd[a, 0] = (part[a, 1, ups].astype(F32) + opp[a, 0].astype(F32)).astype(BF16)
        first_down[a].wait_recv()
        fwd[a, 1] = (part[a, 3, downs].astype(F32) + opp[a, 1].astype(F32)).astype(BF16)
    for a in range(2):
        second_up[a].start()
        second_down[a].start()

    acc[...] = jnp.zeros_like(acc)

    def merge(j, _):
        settle(j, rrecv, rrecv_sem)
        rows = rrecv[j].reshape(ROWS, sub)
        acc[...] += lax.dot_general(onehot[j], rows, TN, preferred_element_type=F32)
        return 0

    lax.fori_loop(0, NZ, merge, 0)
    for h in range(4):
        din_ref[:, h * sub:(h + 1) * sub] = acc[h * tok:(h + 1) * tok, :].astype(BF16)

    for a, out in ((0, dwout_ref), (1, dwin_ref)):
        plain_up[a].wait_recv()
        plain_down[a].wait_recv()
        second_up[a].wait_recv()
        second_down[a].wait_recv()
        out[...] = part[a, 0].astype(F32) + (direct[a, 0].astype(F32) + direct[a, 1].astype(F32))

    def drain(j, _):
        settle(j, send, send_sem)
        settle(j, rsend, rsend_sem)
        return 0

    lax.fori_loop(0, NZ, drain, 0)
    for copy in first_up + first_down + plain_up + plain_down + second_up + second_down:
        copy.wait_send()


def on_device(x, g, eo, w, ids, slots, w1, w2):
    tok, width = x.shape
    sub = w1.shape[1]
    heads = width // sub
    names = tok * heads
    total = NZ * ROWS
    quarter = sub // NY
    vmem = pl.BlockSpec(memory_space=pltpu.VMEM)
    hbm = pl.BlockSpec(memory_space=pl.ANY)
    lanes = lambda v: jnp.transpose(v, (1, 2, 0))
    d_in, d_gates, dw_in, dw_out = pl.pallas_call(
        kernel,
        name="moe_backward",
        out_shape=(
            jax.ShapeDtypeStruct((tok, width), BF16),
            jax.ShapeDtypeStruct((heads, 2, tok), F32),
            jax.ShapeDtypeStruct((quarter, sub), F32),
            jax.ShapeDtypeStruct((quarter, sub), F32),
        ),
        in_specs=[hbm, hbm, hbm, vmem, vmem, vmem, hbm, hbm],
        out_specs=(vmem, vmem, vmem, vmem),
        scratch_shapes=[
            pltpu.VMEM((names, sub), BF16),
            pltpu.VMEM((names, sub), BF16),
            pltpu.VMEM((tok, heads, 2, sub), BF16),
            pltpu.VMEM((sub, sub), BF16),
            pltpu.VMEM((sub, sub), BF16),
            pltpu.VMEM((heads, 2, tok), jnp.int32),
            pltpu.VMEM((NZ, ROWS, names), BF16),
            pltpu.VMEM((NZ, PEERS, 2, CAP, sub), BF16),
            pltpu.VMEM((NZ, PEERS, 2, CAP, sub), BF16),
            pltpu.VMEM((total, sub), BF16),
            pltpu.VMEM((total, sub), BF16),
            pltpu.VMEM((NZ, PEERS, CAP, sub), BF16),
            pltpu.VMEM((NZ, PEERS, CAP, sub), BF16),
            pltpu.VMEM((names, sub), F32),
            pltpu.VMEM((2, NY, quarter, sub), BF16),
            pltpu.VMEM((2, 2, quarter // 2, sub), BF16),
            pltpu.VMEM((2, 2, quarter // 2, sub), BF16),
            pltpu.VMEM((2, 2, quarter, sub), BF16),
            pltpu.SemaphoreType.DMA((3, 4)),
            pltpu.SemaphoreType.DMA((NZ,)),
            pltpu.SemaphoreType.DMA((NZ,)),
            pltpu.SemaphoreType.DMA((NZ,)),
            pltpu.SemaphoreType.DMA((NZ,)),
            pltpu.SemaphoreType.DMA((6, 2)),
            pltpu.SemaphoreType.DMA((2, 2)),
            pltpu.SemaphoreType.DMA((2, 4)),
        ],
        compiler_params=pltpu.CompilerParams(collective_id=0, has_side_effects=True, vmem_limit_bytes=62 << 20),
    )(x, g, eo, lanes(w), lanes(ids), lanes(slots), w1.reshape(sub, sub), w2.reshape(sub, sub))
    return d_in, jnp.transpose(d_gates, (2, 0, 1)), dw_in[None], dw_out[None]


def solution(mesh):
    tokens = P(("expert", "dp"), None)
    per_entry = P(("expert", "dp"), None, None)
    weights = P("expert", None, None)
    in_specs = (tokens, tokens, P(("expert", "dp"), None, None, None)) + (per_entry,) * 3 + (weights,) * 2
    out_specs = (tokens, per_entry, P("expert", "dp", None), P("expert", "dp", None))
    return jax.shard_map(on_device, mesh=mesh, in_specs=in_specs, out_specs=out_specs, check_vma=False)
```

time: 271 us -> 173 us (0.64)
  the two profiles are of different devices: /device:TPU:1 before, /device:TPU:164 now
where the time goes in v1:
time: 173 us
  Pallas kernels  167 us (97%)
  local copies, waits for them, and re-layouts  4.98 us (3%)
    pallas_call x1, Pallas kernels, on_device(): pl.pallas_call(kernel, name='moe_backward', out_shape=(jax.ShapeDtypeStru...  167 us
    unnamed x10, local copies, waits for them, and re-layouts  4.98 us

profile of v1, /device:TPU:164, one launch (start us, length us, event | category | flops | bytes accessed | tf_op | source)
XLA Modules:
  0.0 173.1 jit_solution(14691587379406819955)
XLA Ops:
  0.6 167.5 %moe_backward.1 = (bf16[128,4096]{1,0:T(8,128)(2,1)}, f32[4,2,128]{2,1,0:T(2,128)}, f32[256,1024]{1,0:T(8,128)}, f32[256,1024]{1,0:T(8,128)}) custom-call(bf16[128,4096]{1,0:T(8,128)(2,1)} %x_hbm.1, bf16[128,4096]{1,0:T(8,128)(2,1)} %g_hbm.1, bf16[128,4,2,1024]{3,2,1,0:T(2,128)(2,1)} %eo_hbm.1, f32[4,2,128]{2,1,0:T(2,128)} %bitcast.12, ...), custom_call_target="tpu_custom_call" | custom-call | tf_op jit(solution)/shard_map/moe_backward/pallas_call | solution.py:259
  168.1 0.0 copy-start.2
  168.1 0.0 copy-start.1
  168.1 0.0 copy-start
  168.1 2.4 %copy.16 = bf16[128,4096]{1,0:T(8,128)(2,1)} copy(bf16[128,4096]{1,0:T(8,128)(2,1)} %get-tuple-element.16) | data formatting | bytes 2097152
  170.6 0.0 copy-done.2
  170.6 0.6 copy.17
  171.2 0.0 copy-done.1
  171.2 1.0 copy.18
  172.1 0.0 copy-done
  172.1 1.0 copy.19
Async XLA Ops:
  168.1 2.5 %copy-start.2 = (f32[4,2,128]{2,1,0:T(2,128)S(1)}, f32[4,2,128]{2,1,0:T(2,128)}, u32[]{:S(2)}) copy-start(f32[4,2,128]{2,1,0:T(2,128)} %get-tuple-element.9) | copy-start | bytes 12292
  168.1 3.1 %copy-start.1 = (f32[256,1024]{1,0:T(8,128)S(1)}, f32[256,1024]{1,0:T(8,128)}, u32[]{:S(2)}) copy-start(f32[256,1024]{1,0:T(8,128)} %get-tuple-element.10) | copy-start | bytes 3145732
  168.1 4.0 %copy-start = (f32[256,1024]{1,0:T(8,128)S(1)}, f32[256,1024]{1,0:T(8,128)}, u32[]{:S(2)}) copy-start(f32[256,1024]{1,0:T(8,128)} %get-tuple-element.11) | copy-start | bytes 3145732

commit v2 on v1

--- a/solution.py
+++ b/solution.py
@@ -46,7 +46,7 @@
         pltpu.make_async_copy(w2_hbm, w2, load_sem.at[2, 1]),
         pltpu.make_async_copy(eo_hbm, eo, load_sem.at[2, 2]),
     ]
-    for copy in loads + late:
+    for copy in loads:
         copy.start()
 
     barrier = pltpu.get_barrier_semaphore()
@@ -62,8 +62,9 @@
     tgt[...] = jnp.where(slots_ref[...] >= 0, ids_ref[...] * CAP + slots_ref[...], -1)
 
     def offset_z(j):
-        half = (j + 1) // 2
-        return lax.rem(NZ // 2 + half * (1 - 2 * lax.rem(j, 2)), NZ)
+        k = NZ - 1 - j
+        half = (k + 1) // 2
+        return lax.rem(NZ // 2 + half * (1 - 2 * lax.rem(k, 2)), NZ)
 
     def build(j):
         dz = offset_z(j)
@@ -103,10 +104,10 @@
             device_id=(peer(j, i, -1), y), device_id_type=MESH,
         )
 
-    last = NZ - 1
+    home = 0
 
     def ship(j, copy):
-        @pl.when(j < last)
+        @pl.when(j != home)
         def _():
             copy(j, 0).start()
 
@@ -114,11 +115,11 @@
             copy(j, i).start()
 
     def settle(j, buf, sem):
-        @pl.when(j < last)
+        @pl.when(j != home)
         def _():
             pltpu.make_async_copy(buf.at[j], buf.at[j], sem.at[j]).wait()
 
-        @pl.when(j == last)
+        @pl.when(j == home)
         def _():
             own = buf.at[j, pl.ds(1, PEERS - 1)]
             pltpu.make_async_copy(own, own, sem.at[j]).wait()
@@ -126,16 +127,20 @@
     for copy in loads:
         copy.wait()
     build(0)
+    for copy in late:
+        copy.start()
     pl.semaphore_wait(barrier, NX * NZ * NC - 1 + 2)
+    ship(0, out_copy)
+    build(1)
 
     def dispatch(j, _):
         build(j)
         ship(j - 1, out_copy)
         return 0
 
-    lax.fori_loop(1, NZ, dispatch, 0)
-    recv[last, 0] = send[last, 0]
-    ship(last, out_copy)
+    lax.fori_loop(2, NZ, dispatch, 0)
+    recv[home, 0] = send[home, 0]
+    ship(NZ - 1, out_copy)
 
     late[2].wait()
     for h in range(4):
@@ -169,7 +174,7 @@
         return 0
 
     lax.fori_loop(0, NZ, experts, 0)
-    rrecv[last, 0] = rsend[last, 0]
+    rrecv[home, 0] = rsend[home, 0]
 
     quarter = sub // NY
     half = quarter // 2
@@ -254,7 +259,7 @@
     total = NZ * ROWS
     quarter = sub // NY
     vmem = pl.BlockSpec(memory_space=pltpu.VMEM)
-    hbm = pl.BlockSpec(memory_space=pl.ANY)
+    hbm = pl.BlockSpec(memory_space=pltpu.HBM)
     lanes = lambda v: jnp.transpose(v, (1, 2, 0))
     d_in, d_gates, dw_in, dw_out = pl.pallas_call(
         kernel,
@@ -295,7 +300,7 @@
             pltpu.SemaphoreType.DMA((2, 2)),
             pltpu.SemaphoreType.DMA((2, 4)),
         ],
-        compiler_params=pltpu.CompilerParams(collective_id=0, has_side_effects=True, vmem_limit_bytes=62 << 20),
+        compiler_params=pltpu.CompilerParams(collective_id=0, has_side_effects=True, vmem_limit_bytes=44 << 20),
     )(x, g, eo, lanes(w), lanes(ids), lanes(slots), w1.reshape(sub, sub), w2.reshape(sub, sub))
     return d_in, jnp.transpose(d_gates, (2, 0, 1)), dw_in[None], dw_out[None]
 

time: 173 us -> 169 us (0.977)
  the two profiles are of different devices: /device:TPU:164 before, /device:TPU:1 now
where the time goes in v2:
time: 169 us; the launch traced here: 168 us
  Pallas kernels  156 us (92%)
  local copies, waits for them, and re-layouts  11.2 us (7%)
    pallas_call x1, Pallas kernels, on_device(): pl.pallas_call(kernel, name='moe_backward', out_shape=(jax.ShapeDtypeStru...  156 us
    unnamed x18, local copies, waits for them, and re-layouts  11.2 us

profile of v2, /device:TPU:1, one launch (start us, length us, event | category | flops | bytes accessed | tf_op | source)
XLA Modules:
  0.0 168.3 jit_solution(1093314122062730440)
XLA Ops:
  0.6 0.0 copy-start
  0.6 1.6 copy-done
  2.2 0.0 copy-start.1
  2.2 1.6 copy-done.1
  3.8 0.0 copy-start.2
  3.8 1.2 copy-done.2
  5.0 0.0 copy-start.3
  5.0 1.2 copy-done.3
  6.3 0.0 copy-start.4
  6.3 0.7 copy-done.4
  7.0 0.0 copy-start.5
  7.0 0.7 copy-done.5
  7.6 0.0 copy-start.6
  7.6 0.7 copy-done.6
  8.3 156.5 %moe_backward.1 = (bf16[128,4096]{1,0:T(8,128)(2,1)S(1)}, f32[4,2,128]{2,1,0:T(2,128)S(1)}, f32[256,1024]{1,0:T(8,128)S(1)}, f32[256,1024]{1,0:T(8,128)S(1)}) custom-call(bf16[128,4096]{1,0:T(8,128)(2,1)S(1)} %copy-done.2, bf16[128,4096]{1,0:T(8,128)(2,1)S(1)} %copy-done.3, bf16[128,4,2,1024]{3,2,1,0:T(2,128)(2,1)S(1)} %copy-done, ...), custom_call_target="tpu_custom_call" | custom-call | tf_op jit(solution)/shard_map/moe_backward/pallas_call | solution.py:264
  164.8 1.0 copy.16
  165.8 0.6 copy.17
  166.4 1.0 copy.18
  167.3 1.0 copy.19
Async XLA Ops:
  0.6 1.6 copy-start
  2.2 1.6 copy-start.1
  3.8 1.2 copy-start.2
  5.0 1.2 copy-start.3
  6.3 0.7 copy-start.4
  7.0 0.7 copy-start.5
  7.6 0.7 copy-start.6

commit v3 on v2

--- a/solution.py
+++ b/solution.py
@@ -21,9 +21,9 @@
 
 
 def kernel(
-    x_hbm, g_hbm, eo_hbm, w_ref, ids_ref, slots_ref, w1_hbm, w2_hbm,
+    x_hbm, g_hbm, eo_hbm, w_hbm, ids_hbm, slots_hbm, w1_hbm, w2_hbm,
     din_ref, dgate_ref, dwin_ref, dwout_ref,
-    xs, gs, eo, w1, w2, tgt, onehot, send, recv, hid, grad, rsend, rrecv, acc,
+    xs, gs, eo, w1, w2, w_ref, ids_ref, slots_ref, tgt, onehot, send, recv, hid, grad, rsend, rrecv, acc,
     part, opp, fwd, direct,
     load_sem, send_sem, recv_sem, rsend_sem, rrecv_sem, y_send, y_opp, y_dir,
 ):
@@ -33,6 +33,10 @@
     x, z, c = e // (NZ * NC), lax.rem(e // NC, NZ), lax.rem(e, NC)
     up, down = lax.rem(y + 1, NY), lax.rem(y + NY - 1, NY)
 
+    tables = [
+        pltpu.make_async_copy(src, dst, load_sem.at[3, k])
+        for k, (src, dst) in enumerate(((ids_hbm, ids_ref), (slots_hbm, slots_ref), (w_hbm, w_ref)))
+    ]
     loads = []
     for src, dst, k in ((x_hbm, xs, 0), (g_hbm, gs, 1)):
         for h in range(4):
@@ -46,7 +50,7 @@
         pltpu.make_async_copy(w2_hbm, w2, load_sem.at[2, 1]),
         pltpu.make_async_copy(eo_hbm, eo, load_sem.at[2, 2]),
     ]
-    for copy in loads:
+    for copy in tables + loads:
         copy.start()
 
     barrier = pltpu.get_barrier_semaphore()
@@ -59,6 +63,8 @@
     for other in (up, down):
         pl.semaphore_signal(barrier, inc=1, device_id=(e, other), device_id_type=MESH)
 
+    for copy in tables:
+        copy.wait()
     tgt[...] = jnp.where(slots_ref[...] >= 0, ids_ref[...] * CAP + slots_ref[...], -1)
 
     def offset_z(j):
@@ -265,12 +271,12 @@
         kernel,
         name="moe_backward",
         out_shape=(
-            jax.ShapeDtypeStruct((tok, width), BF16),
-            jax.ShapeDtypeStruct((heads, 2, tok), F32),
-            jax.ShapeDtypeStruct((quarter, sub), F32),
-            jax.ShapeDtypeStruct((quarter, sub), F32),
+            pltpu.VMEM((tok, width), BF16),
+            pltpu.VMEM((heads, 2, tok), F32),
+            pltpu.VMEM((quarter, sub), F32),
+            pltpu.VMEM((quarter, sub), F32),
         ),
-        in_specs=[hbm, hbm, hbm, vmem, vmem, vmem, hbm, hbm],
+        in_specs=[hbm] * 8,
         out_specs=(vmem, vmem, vmem, vmem),
         scratch_shapes=[
             pltpu.VMEM((names, sub), BF16),
@@ -278,6 +284,9 @@
             pltpu.VMEM((tok, heads, 2, sub), BF16),
             pltpu.VMEM((sub, sub), BF16),
             pltpu.VMEM((sub, sub), BF16),
+            pltpu.VMEM((heads, 2, tok), F32),
+            pltpu.VMEM((heads, 2, tok), jnp.int32),
+            pltpu.VMEM((heads, 2, tok), jnp.int32),
             pltpu.VMEM((heads, 2, tok), jnp.int32),
             pltpu.VMEM((NZ, ROWS, names), BF16),
             pltpu.VMEM((NZ, PEERS, 2, CAP, sub), BF16),
@@ -291,7 +300,7 @@
             pltpu.VMEM((2, 2, quarter // 2, sub), BF16),
             pltpu.VMEM((2, 2, quarter // 2, sub), BF16),
             pltpu.VMEM((2, 2, quarter, sub), BF16),
-            pltpu.SemaphoreType.DMA((3, 4)),
+            pltpu.SemaphoreType.DMA((4, 4)),
             pltpu.SemaphoreType.DMA((NZ,)),
             pltpu.SemaphoreType.DMA((NZ,)),
             pltpu.SemaphoreType.DMA((NZ,)),
@@ -300,7 +309,7 @@
             pltpu.SemaphoreType.DMA((2, 2)),
             pltpu.SemaphoreType.DMA((2, 4)),
         ],
-        compiler_params=pltpu.CompilerParams(collective_id=0, has_side_effects=True, vmem_limit_bytes=44 << 20),
+        compiler_params=pltpu.CompilerParams(collective_id=0, has_side_effects=True, vmem_limit_bytes=54 << 20),
     )(x, g, eo, lanes(w), lanes(ids), lanes(slots), w1.reshape(sub, sub), w2.reshape(sub, sub))
     return d_in, jnp.transpose(d_gates, (2, 0, 1)), dw_in[None], dw_out[None]
 

time: 169 us -> 161 us (0.953)
  local copies, waits for them, and re-layouts: 11.2 us -> 3.5 us
    unnamed x18 -> x4, local copies, waits for them, and re-layouts: 11.2 us -> 3.5 us
where the time goes in v3:
time: 161 us; the launch traced here: 160 us
  Pallas kernels  156 us (97%)
  local copies, waits for them, and re-layouts  3.5 us (2%)
    pallas_call x1, Pallas kernels, on_device(): pl.pallas_call(kernel, name='moe_backward', out_shape=(pltpu.VMEM((tok, w...  156 us
    unnamed x4, local copies, waits for them, and re-layouts  3.5 us

profile of v3, /device:TPU:1, one launch (start us, length us, event | category | flops | bytes accessed | tf_op | source)
XLA Modules:
  0.0 160.3 jit_solution(9042569254595538152)
XLA Ops:
  0.6 156.1 %moe_backward.1 = (bf16[128,4096]{1,0:T(8,128)(2,1)S(1)}, f32[4,2,128]{2,1,0:T(2,128)S(1)}, f32[256,1024]{1,0:T(8,128)S(1)}, f32[256,1024]{1,0:T(8,128)S(1)}) custom-call(bf16[128,4096]{1,0:T(8,128)(2,1)} %x_hbm.1, bf16[128,4096]{1,0:T(8,128)(2,1)} %g_hbm.1, bf16[128,4,2,1024]{3,2,1,0:T(2,128)(2,1)} %eo_hbm.1, f32[4,2,128]{2,1,0:T(2,128)} %bitcast.13, ...), custom_call_target="tpu_custom_call" | custom-call | tf_op jit(solution)/shard_map/moe_backward/pallas_call | solution.py:270
  156.8 1.0 copy.16
  157.7 0.6 copy.17
  158.3 1.0 copy.18
  159.3 1.0 copy.19
